TPU v7x, 512 devices: a whole 4x8x8 slice. The times are simulated.
512 devices in a mesh: fluid: 64 (over z, x, core), solid: 8 (over y).
Axes of the slice: x: 4, y: 8, z: 8, core: 2. Of those that a mesh axis runs over, the one named last changes fastest.
Arguments:
- fluid_load: float32 [32768, 3, 128], P(('fluid', 'solid')), may hold values from -6 to 6
- stiffness: float32 [32768, 3, 128], P(('fluid', 'solid')), may hold values from 0.2 to 2
- mapping: bfloat16 [32768, 128, 128], P(('fluid', 'solid')), may hold values from -0.5 to 0.5
- live_count: int32 [512], P(('fluid', 'solid')), may hold values from 40 to 64, as said below
- dest_device: int32 [32768, 1], P(('fluid', 'solid')), may hold values from 0 to 63; in each aligned block of 64 rows (0 to 63, 64 to 127, ...) at most 2 rows name the same one
- local_block: int32 [32768], P(('fluid', 'solid')), may hold values from 0 to 3
- compliance: float32 [8, 256, 3, 128], P('solid', 'fluid'), may hold values from 0.05 to 0.5
- start_disp: float32 [8, 256, 3, 128], P('solid', 'fluid'), may hold values from -40 to 40
- residual_history: float32 [50, 8, 256, 3, 128], P(None, 'solid', 'fluid'), may hold values from -40 to 40
- update_history: float32 [50, 8, 256, 3, 128], P(None, 'solid', 'fluid'), may hold values from -2.4 to 2.4
Outputs:
- displacement: float32 [8, 256, 3, 128], P('solid', 'fluid')
- fluid_displacement: float32 [32768, 3, 128], P(('fluid', 'solid'))
Inputs may be any that keep to these rules, and one draw needn't show every extreme that they name: `live_count`: each device's live blocks are its first ones; some device has exactly 64. `dest_device`: among the 64 rows of one device no fluid index appears more than 2 times.
All inputs are finite; a program needn't handle non-finite values.
Results may differ from a plain program's by a relative error of at most 0.0094.
Values may be sent and summed in bfloat16 or wider, within the bound.
No kernel may reach another device: no remote copies, remote signals or barrier semaphores. Data moves between devices by JAX's collectives and lax.ppermute only.
A program may use at most 64 MiB of HBM per device.

v0:
```python
import jax
import jax.numpy as jnp
from jax import lax
from jax.sharding import Mesh
from jax.sharding import PartitionSpec as P

ITERS = 2
FLUID_SOLID = ("fluid_0", "fluid_1", "fluid_2", "solid")
FLUID = ("fluid_0", "fluid_1", "fluid_2")
ridge_share = 0.01


def over_axes(x, axes):
    for axis in axes:
        x = lax.psum(x, axis)
    return x


def sent_to_all(x, axis):
    copies = jnp.broadcast_to(x, (lax.axis_size(axis), *x.shape))
    return lax.all_to_all(copies, axis, split_axis=0, concat_axis=0, tiled=True)


def in_order(parts, dim):
    dims = list(parts.shape[1:])
    dims[dim] *= parts.shape[0]
    return jnp.moveaxis(parts, 0, dim).reshape(dims)


def gathered_copies(x, axis, dim):
    parts = sent_to_all(x, axis)
    return in_order(parts, dim)


def in_blocks(x, dim, count):
    before, after = (x.shape[:dim], x.shape[dim + 1 :])
    return jnp.moveaxis(x.reshape(*before, count, -1, *after), dim, 0)


def sum_at_owner(x, axis, dim):
    count = lax.axis_size(axis)
    parts = lax.all_to_all(in_blocks(x, dim, count), axis, 0, 0, tiled=True)
    return jnp.sum(parts.astype(jnp.float32), axis=0)


def solve_small(gram_matrix, right_side):
    order = gram_matrix.shape[0]
    ridge = ridge_share * jnp.trace(gram_matrix) / order
    factor = jnp.linalg.cholesky(gram_matrix + ridge * jnp.eye(order, dtype=gram_matrix.dtype))
    halfway = lax.linalg.triangular_solve(factor, right_side[:, None], left_side=True, lower=True)
    solved = lax.linalg.triangular_solve(
        factor, halfway, left_side=True, lower=True, transpose_a=True
    )
    return -solved[:, 0]


def full_sums(basis_flat, resid_flat):
    gram_local = jnp.dot(basis_flat, basis_flat.T, precision=lax.Precision.HIGHEST)
    right_local = jnp.dot(basis_flat, resid_flat, precision=lax.Precision.HIGHEST)
    return (over_axes(gram_local, FLUID_SOLID), over_axes(right_local, FLUID_SOLID))


def body(
    fluid_load,
    stiffness,
    mapping,
    live_count,
    dest_device,
    local_block,
    compliance,
    start_disp,
    residual_history,
    update_history,
):
    blocks = mapping.shape[0]
    sub_blocks = compliance.shape[1]
    alive = (jnp.arange(blocks) < live_count[0]).astype(jnp.float32)[:, None, None]
    target = dest_device[:, 0] * sub_blocks + local_block

    def to_fluid(struct_disp):
        packed = struct_disp[0].astype(jnp.bfloat16)
        pieces = gathered_copies(packed, FLUID, 0)
        onehot = (target[:, None] == jnp.arange(pieces.shape[0])[None, :]).astype(jnp.bfloat16)
        picked = jnp.einsum("bk,kcj->bcj", onehot, pieces, preferred_element_type=jnp.float32)
        fluid_disp = jnp.einsum(
            "bjn,bcj->bcn", mapping, picked.astype(jnp.bfloat16), preferred_element_type=jnp.float32
        )
        return fluid_disp * alive

    struct_disp = start_disp
    basis_cols = residual_history
    updates = update_history
    last_resid = struct_disp
    last_image = struct_disp
    gram_matrix = None
    for iteration in range(ITERS):
        fluid_disp = to_fluid(struct_disp)
        fluid_force = (alive * (fluid_load - stiffness * fluid_disp)).astype(jnp.bfloat16)
        contrib = jnp.einsum(
            "bjn,bcn->bcj", mapping, fluid_force, preferred_element_type=jnp.float32
        )
        force_onehot = (
            jnp.arange(sub_blocks * lax.axis_size(FLUID))[:, None] == target[None, :]
        ).astype(jnp.float32)
        summed = sum_at_owner(
            jnp.einsum(
                "rb,bcj->rcj", force_onehot, contrib, precision=lax.Precision.HIGHEST
            ).astype(jnp.bfloat16),
            FLUID,
            0,
        )
        struct_image = compliance * summed[None]
        residual = struct_image - struct_disp
        newest = residual - last_resid
        if iteration > 0:
            basis_cols = jnp.concatenate([basis_cols[1:], newest[None]], 0)
            updates = jnp.concatenate([updates[1:], (struct_image - last_image)[None]], 0)
        basis_flat = basis_cols.reshape(basis_cols.shape[0], -1)
        resid_flat = residual.reshape(-1)
        if iteration == 0:
            gram_matrix, right_side = full_sums(basis_flat, resid_flat)
        else:
            row_local = jnp.dot(basis_flat, newest.reshape(-1), precision=lax.Precision.HIGHEST)
            right_local = jnp.dot(basis_flat, resid_flat, precision=lax.Precision.HIGHEST)
            new_row, right_side = (
                over_axes(row_local, FLUID_SOLID),
                over_axes(right_local, FLUID_SOLID),
            )
            upper_part = jnp.concatenate([gram_matrix[1:, 1:], new_row[:-1, None]], 1)
            gram_matrix = jnp.concatenate([upper_part, new_row[None, :]], 0)
        coefficients = solve_small(gram_matrix, right_side)
        struct_disp = struct_image + jnp.tensordot(
            coefficients, updates, axes=1, precision=lax.Precision.HIGHEST
        )
        last_resid = residual
        last_image = struct_image
    final_disp = to_fluid(struct_disp)
    return (struct_disp, final_disp)


def solution(mesh):
    split = Mesh(
        mesh.devices.reshape(8, 4, 2, mesh.shape["solid"]),
        ("fluid_0", "fluid_1", "fluid_2", "solid"),
    )
    in_specs = (
        P(FLUID_SOLID, None, None),
        P(FLUID_SOLID, None, None),
        P(FLUID_SOLID, None, None),
        P(FLUID_SOLID),
        P(FLUID_SOLID, None),
        P(FLUID_SOLID),
        P("solid", FLUID, None, None),
        P("solid", FLUID, None, None),
        P(None, "solid", FLUID, None, None),
        P(None, "solid", FLUID, None, None),
    )
    out_specs = (P("solid", FLUID, None, None), P(FLUID_SOLID, None, None))
    return jax.shard_map(body, mesh=split, in_specs=in_specs, out_specs=out_specs, check_vma=False)
```

profile of v0, /device:TPU:1, one launch (start us, length us, event | category | flops | bytes accessed | tf_op | source)
XLA Modules:
  0.0 251.1 jit_solution(15389651478953611320)
XLA Ops:
  0.6 0.8 convert_bitcast_fusion.2
  1.5 0.7 broadcast_in_dim.50
  2.2 14.8 %all-to-all-start = ((bf16[64,4,3,128]{3,1,2,0:T(4,128)(2,1)}), bf16[64,4,3,128]{3,1,2,0:T(4,128)(2,1)S(1)}, u32[]{:S(2)}, u32[]{:S(2)}) async-start(bf16[64,4,3,128]{3,1,2,0:T(4,128)(2,1)} %broadcast_in_dim.50), calls=%async_computation | async-start | bytes 393216 | tf_op jit(solution)/shard_map/all_to_all | solution.py:21
  17.7 0.7 bitcast_add_fusion.2
  18.4 10.7 %all-to-all-done = bf16[64,4,3,128]{3,1,2,0:T(4,128)(2,1)S(1)} async-done(((bf16[64,4,3,128]{3,1,2,0:T(4,128)(2,1)}), bf16[64,4,3,128]{3,1,2,0:T(4,128)(2,1)S(1)}, u32[]{:S(2)}, u32[]{:S(2)}) %all-to-all-start) | async-done | bytes 196640 | tf_op jit(solution)/shard_map/all_to_all | solution.py:21
  29.0 0.1 copy.39
  29.1 0.2 convolution_convert_fusion.4
  29.4 2.7 %fusion.9 = f32[64,3,128]{2,1,0:T(4,128)S(1)} fusion(bf16[64,128,128]{2,1,0:T(8,128)(2,1)S(1)} %copy-done, f32[64,3,128]{2,0,1:T(8,128)} %param.15, f32[64,3,128]{2,0,1:T(8,128)} %param.16, bf16[64,3,128]{2,0,1:T(8,128)(2,1)S(1)} %convolution_convert_fusion.4, f32[64]{0:T(128)S(1)} %compare_convert_fusion), kind=kOutput, calls=%fused_computation.17 | convolution fusion | flops 12705792 | bytes 2441472 | tf_op jit(solution)/shard_map/bjn,bcn->bcj/dot_general | solution.py:99
  32.1 0.5 convolution_convert_fusion.1
  32.5 0.7 copy.44
  33.3 4.5 %all-to-all-start.1 = ((bf16[64,4,3,128]{3,1,2,0:T(4,128)(2,1)}), bf16[64,4,3,128]{3,1,2,0:T(4,128)(2,1)S(1)}, u32[]{:S(2)}, u32[]{:S(2)}) async-start(bf16[64,4,3,128]{3,1,2,0:T(4,128)(2,1)} %copy.44), calls=%async_computation.1 | async-start | bytes 393216 | tf_op jit(solution)/shard_map/all_to_all | solution.py:42
  37.8 0.4 convolution_bitcast_fusion
  38.2 11.7 %all-to-all-done.1 = bf16[64,4,3,128]{3,1,2,0:T(4,128)(2,1)S(1)} async-done(((bf16[64,4,3,128]{3,1,2,0:T(4,128)(2,1)}), bf16[64,4,3,128]{3,1,2,0:T(4,128)(2,1)S(1)}, u32[]{:S(2)}, u32[]{:S(2)}) %all-to-all-start.1) | async-done | bytes 196640 | tf_op jit(solution)/shard_map/all_to_all | solution.py:42
  49.9 0.1 convert_reduce_fusion.1
  50.1 0.4 convolution_bitcast_fusion.3
  50.4 21.0 %all-reduce.3 = (f32[50]{0:T(128)S(1)}, f32[50,50]{0,1:T(8,128)S(1)}) all-reduce(f32[50]{0:T(128)S(1)} %convolution_bitcast_fusion.3, f32[50,50]{0,1:T(8,128)S(1)} %convolution_bitcast_fusion), channel_id=1, replica_groups=mesh['fluid_0'=8,'fluid_1'=4,'fluid_2'=2,'solid'=8] {'fluid_0'}, use_global_device_ids=true, to_apply=%region_8.10 | all-reduce | flops 2550 | bytes 20400 | tf_op jit(solution)/shard_map/psum | solution.py:15
  71.4 11.7 %all-reduce.5 = (f32[50]{0:T(128)S(1)}, f32[50,50]{0,1:T(8,128)S(1)}) all-reduce(f32[50]{0:T(128)S(1)} %get-tuple-element.17, f32[50,50]{0,1:T(8,128)S(1)} %get-tuple-element.18), channel_id=1, replica_groups=mesh['fluid_0'=8,'fluid_1'=4,'fluid_2'=2,'solid'=8] {'fluid_1'}, use_global_device_ids=true, to_apply=%region_9.0 | all-reduce | flops 2550 | bytes 20400 | tf_op jit(solution)/shard_map/psum | solution.py:15
  83.1 14.6 %all-reduce.7 = (f32[50]{0:T(128)S(1)}, f32[50,50]{0,1:T(8,128)S(1)}) all-reduce(f32[50]{0:T(128)S(1)} %get-tuple-element.21, f32[50,50]{0,1:T(8,128)S(1)} %get-tuple-element.22), channel_id=1, replica_groups=mesh['fluid_0'=8,'fluid_1'=4,'fluid_2'=2,'solid'=8] {'fluid_2'}, use_global_device_ids=true, to_apply=%region_10.12 | all-reduce | flops 2550 | bytes 20400 | tf_op jit(solution)/shard_map/psum | solution.py:15
  97.7 23.2 %all-reduce.1 = (f32[50,1]{0,1:T(1,128)S(1)}, f32[50,50]{0,1:T(8,128)S(1)}) all-reduce(f32[50,1]{0,1:T(1,128)S(1)} %bitcast.163, f32[50,50]{0,1:T(8,128)S(1)} %get-tuple-element.26), channel_id=1, replica_groups=mesh['fluid_0'=8,'fluid_1'=4,'fluid_2'=2,'solid'=8] {'solid'}, use_global_device_ids=true, to_apply=%region_11.13 | all-reduce | flops 2550 | bytes 20400 | tf_op jit(solution)/shard_map/psum | solution.py:15
  120.9 0.6 select_reduce_fusion.3
  122.1 0.1 copy.48
  122.3 4.6 %cholesky.44 = f32[50,50]{1,0:T(8,128)S(1)} custom-call(f32[50,50]{1,0:T(8,128)S(1)} %fusion.54), custom_call_target="Cholesky" | custom-call | tf_op jit(solution)/shard_map/jit(cholesky)/cholesky | solution.py:49
  126.9 0.6 compare_reduce_fusion.1
  127.5 0.7 fusion.47
  128.2 3.8 %custom-call.11 = f32[1,50,50]{1,2,0:T(8,128)S(1)} custom-call(f32[1,50,50]{2,1,0:T(8,128)S(1)} %fusion.47), custom_call_target="InvertDiagBlocksLowerTriangular" | custom-call | tf_op jit(solution)/shard_map/triangular_solve/custom-call.2 | solution.py:51
  132.0 0.2 convolution_bitcast_fusion.7
  132.1 0.2 fusion.13
  132.3 0.3 fusion.16
  132.7 24.8 %all_to_all.25 = bf16[64,4,3,128]{3,1,2,0:T(4,128)(2,1)S(1)} all-to-all(bf16[64,4,3,128]{3,1,2,0:T(4,128)(2,1)S(1)} %broadcast_in_dim.54), channel_id=1, replica_groups=mesh['fluid_0'=8,'fluid_1'=4,'fluid_2'=2,'solid'=8] {'fluid_0','fluid_1'..., dimensions={0} | all-to-all | bytes 393216 | tf_op jit(solution)/shard_map/all_to_all | solution.py:21
  157.5 0.1 copy.49
  157.6 0.2 convolution_convert_fusion.3
  157.8 1.7 fusion.8
  159.6 0.5 convolution_convert_fusion
  160.0 0.7 copy.54
  160.8 4.5 %all-to-all-start.3 = ((bf16[64,4,3,128]{3,1,2,0:T(4,128)(2,1)}), bf16[64,4,3,128]{3,1,2,0:T(4,128)(2,1)S(1)}, u32[]{:S(2)}, u32[]{:S(2)}) async-start(bf16[64,4,3,128]{3,1,2,0:T(4,128)(2,1)} %copy.54), calls=%async_computation.3 | async-start | bytes 393216 | tf_op jit(solution)/shard_map/all_to_all | solution.py:42
  165.3 0.1 slice.24
  165.4 12.0 %all-to-all-done.3 = bf16[64,4,3,128]{3,1,2,0:T(4,128)(2,1)S(1)} async-done(((bf16[64,4,3,128]{3,1,2,0:T(4,128)(2,1)}), bf16[64,4,3,128]{3,1,2,0:T(4,128)(2,1)S(1)}, u32[]{:S(2)}, u32[]{:S(2)}) %all-to-all-start.3) | async-done | bytes 196640 | tf_op jit(solution)/shard_map/all_to_all | solution.py:42
  177.4 0.1 convert_reduce_fusion
  177.5 0.1 maximum_bitcast_fusion
  177.6 0.4 convolution_bitcast_fusion.1
  178.0 0.4 convolution_bitcast_fusion.2
  178.4 11.9 %all-reduce.2 = (f32[50]{0:T(128)S(1)}, f32[50]{0:T(128)S(1)}) all-reduce(f32[50]{0:T(128)S(1)} %convolution_bitcast_fusion.1, f32[50]{0:T(128)S(1)} %convolution_bitcast_fusion.2), channel_id=1, replica_groups=mesh['fluid_0'=8,'fluid_1'=4,'fluid_2'=2,'solid'=8] {'fluid_0'}, use_global_device_ids=true, to_apply=%region_18.0 | all-reduce | flops 100 | bytes 800 | tf_op jit(solution)/shard_map/psum | solution.py:15
  190.2 6.5 %all-reduce.4 = (f32[50]{0:T(128)S(1)}, f32[50]{0:T(128)S(1)}) all-reduce(f32[50]{0:T(128)S(1)} %get-tuple-element.15, f32[50]{0:T(128)S(1)} %get-tuple-element.16), channel_id=1, replica_groups=mesh['fluid_0'=8,'fluid_1'=4,'fluid_2'=2,'solid'=8] {'fluid_1'}, use_global_device_ids=true, to_apply=%region_19.23 | all-reduce | flops 100 | bytes 800 | tf_op jit(solution)/shard_map/psum | solution.py:15
  196.8 8.5 %all-reduce.6 = (f32[50]{0:T(128)S(1)}, f32[50]{0:T(128)S(1)}) all-reduce(f32[50]{0:T(128)S(1)} %get-tuple-element.19, f32[50]{0:T(128)S(1)} %get-tuple-element.20), channel_id=1, replica_groups=mesh['fluid_0'=8,'fluid_1'=4,'fluid_2'=2,'solid'=8] {'fluid_2'}, use_global_device_ids=true, to_apply=%region_20.24 | all-reduce | flops 100 | bytes 800 | tf_op jit(solution)/shard_map/psum | solution.py:15
  205.3 10.8 %all-reduce = (f32[50,1]{0,1:T(1,128)S(1)}, f32[50]{0:T(128)S(1)}) all-reduce(f32[50,1]{0,1:T(1,128)S(1)} %bitcast.165, f32[50]{0:T(128)S(1)} %get-tuple-element.24), channel_id=1, replica_groups=mesh['fluid_0'=8,'fluid_1'=4,'fluid_2'=2,'solid'=8] {'solid'}, use_global_device_ids=true, to_apply=%region_21.25 | all-reduce | flops 100 | bytes 800 | tf_op jit(solution)/shard_map/psum | solution.py:15
  216.0 0.1 copy.55
  216.1 0.7 select_reduce_fusion.2
  217.5 0.1 select_add_fusion
  217.6 0.1 copy.56
  217.7 0.1 fusion.51
  217.7 4.6 %cholesky.55 = f32[50,50]{1,0:T(8,128)S(1)} custom-call(f32[50,50]{1,0:T(8,128)S(1)} %fusion.51), custom_call_target="Cholesky" | custom-call | tf_op jit(solution)/shard_map/jit(cholesky)/cholesky | solution.py:49
  222.3 0.6 compare_reduce_fusion
  223.0 0.7 fusion.48
  223.6 3.8 %custom-call.13 = f32[1,50,50]{1,2,0:T(8,128)S(1)} custom-call(f32[1,50,50]{2,1,0:T(8,128)S(1)} %fusion.48), custom_call_target="InvertDiagBlocksLowerTriangular" | custom-call | tf_op jit(solution)/shard_map/triangular_solve/custom-call.2 | solution.py:51
  227.5 0.2 convolution_bitcast_fusion.5
  227.6 0.2 fusion.11
  227.8 0.1 maximum_bitcast_fusion.1
  227.9 0.3 fusion.14
  228.2 0.6 convert_bitcast_fusion
  228.8 20.7 %all_to_all.26 = bf16[64,4,3,128]{3,1,2,0:T(4,128)(2,1)S(1)} all-to-all(bf16[64,4,3,128]{3,1,2,0:T(4,128)(2,1)S(1)} %broadcast_in_dim.61), channel_id=1, replica_groups=mesh['fluid_0'=8,'fluid_1'=4,'fluid_2'=2,'solid'=8] {'fluid_0','fluid_1'..., dimensions={0} | all-to-all | bytes 393216 | tf_op jit(solution)/shard_map/all_to_all | solution.py:21
  249.6 0.1 copy.57
  249.6 0.2 convolution_convert_fusion.2
  249.8 0.7 convolution_multiply_fusion
  250.5 0.7 copy.59
  (28 shorter events, 0.3 us)
Async XLA Ops:
  0.6 28.7 %copy-start = (bf16[64,128,128]{2,1,0:T(8,128)(2,1)S(1)}, bf16[64,128,128]{2,1,0:T(8,128)(2,1)}, u32[]{:S(2)}) copy-start(bf16[64,128,128]{2,1,0:T(8,128)(2,1)} %param.17) | copy-start | bytes 6291460
  2.2 26.8 %all-to-all-start = ((bf16[64,4,3,128]{3,1,2,0:T(4,128)(2,1)}), bf16[64,4,3,128]{3,1,2,0:T(4,128)(2,1)S(1)}, u32[]{:S(2)}, u32[]{:S(2)}) async-start(bf16[64,4,3,128]{3,1,2,0:T(4,128)(2,1)} %broadcast_in_dim.50), calls=%async_computation | async-start | bytes 393216 | tf_op jit(solution)/shard_map/all_to_all | solution.py:21
  29.3 8.4 %copy-start.1 = (f32[50,1,4,3,128]{4,2,3,1,0:T(4,128)S(1)}, f32[50,1,4,3,128]{4,2,3,1,0:T(4,128)}, u32[]{:S(2)}) copy-start(f32[50,1,4,3,128]{4,2,3,1,0:T(4,128)} %param.23) | copy-start | bytes 921604
  29.4 20.7 %copy-start.5 = (f32[1,4,3,128]{3,1,2,0:T(4,128)S(1)}, f32[1,4,3,128]{3,1,2,0:T(4,128)}, u32[]{:S(2)}) copy-start(f32[1,4,3,128]{3,1,2,0:T(4,128)} %param.21) | copy-start | bytes 18436
  29.4 20.7 %copy-start.6 = (f32[1,4,3,128]{3,1,2,0:T(4,128)S(1)}, f32[1,4,3,128]{3,1,2,0:T(4,128)}, u32[]{:S(2)}) copy-start(f32[1,4,3,128]{3,1,2,0:T(4,128)} %param.22) | copy-start | bytes 18436
  32.1 100.2 %copy-start.2 = (f32[50,1,4,3,128]{4,2,3,1,0:T(4,128)S(1)}, f32[50,1,4,3,128]{4,2,3,1,0:T(4,128)}, u32[]{:S(2)}) copy-start(f32[50,1,4,3,128]{4,2,3,1,0:T(4,128)} %param.24) | copy-start | bytes 921604
  32.1 125.8 %copy-start.3 = (f32[64,3,128]{2,0,1:T(8,128)S(1)}, f32[64,3,128]{2,0,1:T(8,128)}, u32[]{:S(2)}) copy-start(f32[64,3,128]{2,0,1:T(8,128)} %param.15) | copy-start | bytes 294916
  32.1 125.8 %copy-start.4 = (f32[64,3,128]{2,0,1:T(8,128)S(1)}, f32[64,3,128]{2,0,1:T(8,128)}, u32[]{:S(2)}) copy-start(f32[64,3,128]{2,0,1:T(8,128)} %param.16) | copy-start | bytes 294916
  33.3 16.6 %all-to-all-start.1 = ((bf16[64,4,3,128]{3,1,2,0:T(4,128)(2,1)}), bf16[64,4,3,128]{3,1,2,0:T(4,128)(2,1)S(1)}, u32[]{:S(2)}, u32[]{:S(2)}) async-start(bf16[64,4,3,128]{3,1,2,0:T(4,128)(2,1)} %copy.44), calls=%async_computation.1 | async-start | bytes 393216 | tf_op jit(solution)/shard_map/all_to_all | solution.py:42
  160.8 16.6 %all-to-all-start.3 = ((bf16[64,4,3,128]{3,1,2,0:T(4,128)(2,1)}), bf16[64,4,3,128]{3,1,2,0:T(4,128)(2,1)S(1)}, u32[]{:S(2)}, u32[]{:S(2)}) async-start(bf16[64,4,3,128]{3,1,2,0:T(4,128)(2,1)} %copy.54), calls=%async_computation.3 | async-start | bytes 393216 | tf_op jit(solution)/shard_map/all_to_all | solution.py:42
where the time goes:
time: 252 us; the launch traced here: 251 us
  blocking collectives  154 us (61%)
  waiting for transfers between devices  34.4 us (14%)
  starting transfers between devices  23.8 us (9%)
  other arithmetic  23.5 us (9%)
  matrix products  9.37 us (4%)
  local copies, waits for them, and re-layouts  3.67 us (1%)
  between operations  2.85 us (1%)
    psum x8, blocking collectives, over_axes(): x = lax.psum(x, axis)  108 us
    all_to_all x2, blocking collectives, sent_to_all(): return lax.all_to_all(copies, axis, split_axis=0, concat_axis=0, tiled=True)  45.6 us
    all_to_all x2, waiting for transfers between devices, sum_at_owner(): parts = lax.all_to_all(in_blocks(x, dim, count), axis, 0, 0, tiled=True)  23.7 us
    all_to_all x1, starting transfers between devices, sent_to_all(): return lax.all_to_all(copies, axis, split_axis=0, concat_axis=0, tiled=True)  14.8 us
    all_to_all x1, waiting for transfers between devices, sent_to_all(): return lax.all_to_all(copies, axis, split_axis=0, concat_axis=0, tiled=True)  10.7 us
    another operation x6, other arithmetic, solve_small(): jnp.linalg.cholesky(gram_matrix + ridge * jnp.eye(order, dtype=gram_matri...  10.5 us
    another operation x4, other arithmetic, solve_small(): lax.linalg.triangular_solve(factor, halfway, left_side=True, lower=True,...  8.96 us
    all_to_all x2, starting transfers between devices, sum_at_owner(): parts = lax.all_to_all(in_blocks(x, dim, count), axis, 0, 0, tiled=True)  8.93 us
  transfers between devices with their start and end apart: 3, of which 3 were waited for; matrix products, arithmetic and copies ran while one was open for 0% of the time, Pallas kernels for 0%

commit v1 on v0

--- a/solution.py
+++ b/solution.py
@@ -12,7 +12,7 @@
 
 def over_axes(x, axes):
     for axis in axes:
-        x = lax.psum(x, axis)
+        x = lax.all_gather(x, axis_name=axis).sum(axis=0)
     return x
 
 

time: 252 us -> 281 us (1.12)
  blocking collectives: 154 us -> 183 us
  waiting for transfers between devices: 34.4 us -> 12.1 us
  starting transfers between devices: 23.8 us -> 34.2 us
  local copies, waits for them, and re-layouts: 3.67 us -> 12.8 us
    psum x8 -> x0, blocking collectives: 108 us -> none  [over_axes(): x = lax.psum(x, axis)]
    unnamed x0 -> x8, blocking collectives: none -> 80.1 us
    all_gather x0 -> x4, blocking collectives: none -> 60.2 us  [over_axes(): x = lax.all_gather(x, axis_name=axis).sum(axis=0)]
    all_to_all x2, waiting for transfers between devices: 23.7 us -> 12.1 us  [sum_at_owner(): parts = lax.all_to_all(in_blocks(x, dim, count), axis, 0, 0, tiled=True)]
    all_to_all x1, waiting for transfers between devices: 10.7 us -> 0.01 us  [sent_to_all(): return lax.all_to_all(copies, axis, split_axis=0, concat_axis=0, tiled=True)]
    all_to_all x2, starting transfers between devices: 8.93 us -> 19.4 us  [sum_at_owner(): parts = lax.all_to_all(in_blocks(x, dim, count), axis, 0, 0, tiled=True)]
    unnamed x15 -> x47, local copies, waits for them, and re-layouts: 0.7 us -> 8.7 us
    all_to_all x2, blocking collectives: 45.6 us -> 42.2 us  [sent_to_all(): return lax.all_to_all(copies, axis, split_axis=0, concat_axis=0, tiled=True)]
  transfers between devices with their start and end apart: 3 -> 3, of which waited for: 3 -> 1; matrix products, arithmetic and copies ran while one was open for 0% -> 6% of each run, Pallas kernels for 0% -> 0%
where the time goes in v1:
time: 281 us; the launch traced here: 280 us
  blocking collectives  183 us (65%)
  starting transfers between devices  34.2 us (12%)
  other arithmetic  23.1 us (8%)
  local copies, waits for them, and re-layouts  12.8 us (5%)
  waiting for transfers between devices  12.1 us (4%)
  matrix products  9.43 us (3%)
  between operations  5.55 us (2%)
    unnamed x8, blocking collectives  80.1 us
    all_gather x4, blocking collectives, over_axes(): x = lax.all_gather(x, axis_name=axis).sum(axis=0)  60.2 us
    all_to_all x2, blocking collectives, sent_to_all(): return lax.all_to_all(copies, axis, split_axis=0, concat_axis=0, tiled=True)  42.2 us
    all_to_all x2, starting transfers between devices, sum_at_owner(): parts = lax.all_to_all(in_blocks(x, dim, count), axis, 0, 0, tiled=True)  19.4 us
    all_to_all x1, starting transfers between devices, sent_to_all(): return lax.all_to_all(copies, axis, split_axis=0, concat_axis=0, tiled=True)  14.8 us
    all_to_all x2, waiting for transfers between devices, sum_at_owner(): parts = lax.all_to_all(in_blocks(x, dim, count), axis, 0, 0, tiled=True)  12.1 us
    another operation x6, other arithmetic, solve_small(): jnp.linalg.cholesky(gram_matrix + ridge * jnp.eye(order, dtype=gram_matri...  10.5 us
    another operation x4, other arithmetic, solve_small(): lax.linalg.triangular_solve(factor, halfway, left_side=True, lower=True,...  8.96 us
  transfers between devices with their start and end apart: 3, of which 1 were waited for; matrix products, arithmetic and copies ran while one was open for 6% of the time, Pallas kernels for 0%

profile of v1, /device:TPU:1, one launch (start us, length us, event | category | flops | bytes accessed | tf_op | source)
XLA Modules:
  0.0 279.8 jit_solution(9695604765951043781)
XLA Ops:
  0.7 0.8 convert_bitcast_fusion.2
  1.5 0.7 broadcast_in_dim.50
  2.3 14.8 %all-to-all-start = ((bf16[64,4,3,128]{3,1,2,0:T(4,128)(2,1)}), bf16[64,4,3,128]{3,1,2,0:T(4,128)(2,1)S(1)}, u32[]{:S(2)}, u32[]{:S(2)}) async-start(bf16[64,4,3,128]{3,1,2,0:T(4,128)(2,1)} %broadcast_in_dim.50), calls=%async_computation | async-start | bytes 393216 | tf_op jit(solution)/shard_map/all_to_all | solution.py:21
  17.1 1.5 convolution_bitcast_fusion
  18.6 20.6 %all-gather.16 = f32[8,50,50]{2,1,0:T(8,128)S(1)} all-gather(f32[1,50,50]{2,1,0:T(8,128)S(1)} %convolution_bitcast_fusion), channel_id=2, replica_groups=mesh['fluid_0'=8,'fluid_1'=4,'fluid_2'=2,'solid'=8] {'fluid_0'}, dimensions={0}, use_global_device_ids=true | all-gather | bytes 90000 | tf_op jit(solution)/shard_map/all_gather | solution.py:15
  39.2 9.3 %all-gather.17 = f32[4,50,50]{2,1,0:T(8,128)S(1)} all-gather(f32[1,50,50]{2,1,0:T(8,128)S(1)} %bitcast.174), channel_id=3, replica_groups=mesh['fluid_0'=8,'fluid_1'=4,'fluid_2'=2,'solid'=8] {'fluid_1'}, dimensions={0}, use_global_device_ids=true | all-gather | bytes 50000 | tf_op jit(solution)/shard_map/all_gather | solution.py:15
  48.5 10.3 %all-gather.18 = f32[2,50,50]{2,1,0:T(8,128)S(1)} all-gather(f32[1,50,50]{2,1,0:T(8,128)S(1)} %bitcast.175), channel_id=4, replica_groups=mesh['fluid_0'=8,'fluid_1'=4,'fluid_2'=2,'solid'=8] {'fluid_2'}, dimensions={0}, use_global_device_ids=true | all-gather | bytes 30000 | tf_op jit(solution)/shard_map/all_gather | solution.py:15
  58.9 20.0 %all-gather.19 = f32[8,50,50]{2,1,0:T(8,128)S(1)} all-gather(f32[1,50,50]{2,1,0:T(8,128)S(1)} %bitcast.176), channel_id=5, replica_groups=mesh['fluid_0'=8,'fluid_1'=4,'fluid_2'=2,'solid'=8] {'solid'}, dimensions={0}, use_global_device_ids=true | all-gather | bytes 90000 | tf_op jit(solution)/shard_map/all_gather | solution.py:15
  79.0 0.6 select_reduce_fusion.3
  80.4 4.6 %cholesky.44 = f32[50,50]{1,0:T(8,128)S(1)} custom-call(f32[50,50]{1,0:T(8,128)S(1)} %fusion.54), custom_call_target="Cholesky" | custom-call | tf_op jit(solution)/shard_map/jit(cholesky)/cholesky | solution.py:49
  85.7 0.2 convolution_convert_fusion.4
  86.0 1.7 fusion.9
  87.7 0.5 convolution_convert_fusion.1
  88.2 0.7 copy.85
  88.9 14.8 %all-to-all-start.1 = ((bf16[64,4,3,128]{3,1,2,0:T(4,128)(2,1)}), bf16[64,4,3,128]{3,1,2,0:T(4,128)(2,1)S(1)}, u32[]{:S(2)}, u32[]{:S(2)}) async-start(bf16[64,4,3,128]{3,1,2,0:T(4,128)(2,1)} %copy.85), calls=%async_computation.1 | async-start | bytes 393216 | tf_op jit(solution)/shard_map/all_to_all | solution.py:42
  103.8 0.6 compare_reduce_fusion.1
  104.4 0.7 fusion.47
  105.1 3.8 %custom-call.11 = f32[1,50,50]{1,2,0:T(8,128)S(1)} custom-call(f32[1,50,50]{2,1,0:T(8,128)S(1)} %fusion.47), custom_call_target="InvertDiagBlocksLowerTriangular" | custom-call | tf_op jit(solution)/shard_map/triangular_solve/custom-call.2 | solution.py:51
  108.9 1.3 dynamic-slice
  110.2 1.3 dynamic-slice.1
  112.7 1.3 dynamic-slice.2
  114.7 1.3 dynamic-slice.3
  116.8 0.4 convolution_bitcast_fusion.3
  117.2 0.2 dynamic-update-slice.2
  117.4 13.5 %all-reduce = f32[400]{0:T(512)S(1)} all-reduce(f32[400]{0:T(512)S(1)} %dynamic-update-slice.2), channel_id=6, replica_groups=mesh['fluid_0'=8,'fluid_1'=4,'fluid_2'=2,'solid'=8] {'fluid_0'}, use_global_device_ids=true, to_apply=%add | all-reduce | flops 400 | bytes 3200
  131.0 0.2 dynamic-update-slice.3
  131.2 8.4 %all-reduce.1 = f32[200]{0:T(256)S(1)} all-reduce(f32[200]{0:T(256)S(1)} %dynamic-update-slice.3), channel_id=7, replica_groups=mesh['fluid_0'=8,'fluid_1'=4,'fluid_2'=2,'solid'=8] {'fluid_1'}, use_global_device_ids=true, to_apply=%add.1 | all-reduce | flops 200 | bytes 1600
  139.7 0.2 dynamic-update-slice.4
  140.0 8.3 %all-reduce.2 = f32[100]{0:T(128)S(1)} all-reduce(f32[100]{0:T(128)S(1)} %dynamic-update-slice.4), channel_id=8, replica_groups=mesh['fluid_0'=8,'fluid_1'=4,'fluid_2'=2,'solid'=8] {'fluid_2'}, use_global_device_ids=true, to_apply=%add.2 | all-reduce | flops 100 | bytes 800
  148.3 0.2 dynamic-update-slice.5
  148.6 12.2 %all-reduce.3 = f32[400]{0:T(512)S(1)} all-reduce(f32[400]{0:T(512)S(1)} %dynamic-update-slice.5), channel_id=9, replica_groups=mesh['fluid_0'=8,'fluid_1'=4,'fluid_2'=2,'solid'=8] {'solid'}, use_global_device_ids=true, to_apply=%add.3 | all-reduce | flops 400 | bytes 3200
  161.1 0.3 fusion.16
  161.5 21.2 %all_to_all.25 = bf16[64,4,3,128]{3,1,2,0:T(4,128)(2,1)S(1)} all-to-all(bf16[64,4,3,128]{3,1,2,0:T(4,128)(2,1)S(1)} %broadcast_in_dim.54), channel_id=1, replica_groups=mesh['fluid_0'=8,'fluid_1'=4,'fluid_2'=2,'solid'=8] {'fluid_0','fluid_1'..., dimensions={0} | all-to-all | bytes 393216 | tf_op jit(solution)/shard_map/all_to_all | solution.py:21
  182.8 0.2 convolution_convert_fusion.3
  183.0 1.7 fusion.8
  184.7 0.5 convolution_convert_fusion
  185.2 0.7 copy.96
  185.9 4.6 %all-to-all-start.3 = ((bf16[64,4,3,128]{3,1,2,0:T(4,128)(2,1)}), bf16[64,4,3,128]{3,1,2,0:T(4,128)(2,1)S(1)}, u32[]{:S(2)}, u32[]{:S(2)}) async-start(bf16[64,4,3,128]{3,1,2,0:T(4,128)(2,1)} %copy.96), calls=%async_computation.3 | async-start | bytes 393216 | tf_op jit(solution)/shard_map/all_to_all | solution.py:42
  190.7 12.1 %all-to-all-done.3 = bf16[64,4,3,128]{3,1,2,0:T(4,128)(2,1)S(1)} async-done(((bf16[64,4,3,128]{3,1,2,0:T(4,128)(2,1)}), bf16[64,4,3,128]{3,1,2,0:T(4,128)(2,1)S(1)}, u32[]{:S(2)}, u32[]{:S(2)}) %all-to-all-start.3) | async-done | bytes 196640 | tf_op jit(solution)/shard_map/all_to_all | solution.py:42
  203.0 0.4 convolution_bitcast_fusion.1
  203.4 0.4 convolution_bitcast_fusion.2
  203.8 0.2 dynamic-update-slice.10
  204.0 0.2 dynamic-update-slice.6
  204.2 11.3 %all-reduce.13 = (f32[400]{0:T(512)S(1)}, f32[400]{0:T(512)S(1)}) all-reduce(f32[400]{0:T(512)S(1)} %dynamic-update-slice.6, f32[400]{0:T(512)S(1)} %dynamic-update-slice.10), channel_id=10, replica_groups=mesh['fluid_0'=8,'fluid_1'=4,'fluid_2'=2,'solid'=8] {'fluid_0'}, use_global_device_ids=true, to_apply=%add.4 | all-reduce | flops 800 | bytes 6400
  215.7 0.2 dynamic-update-slice.11
  215.9 0.2 dynamic-update-slice.7
  216.2 6.8 %all-reduce.14 = (f32[200]{0:T(256)S(1)}, f32[200]{0:T(256)S(1)}) all-reduce(f32[200]{0:T(256)S(1)} %dynamic-update-slice.7, f32[200]{0:T(256)S(1)} %dynamic-update-slice.11), channel_id=11, replica_groups=mesh['fluid_0'=8,'fluid_1'=4,'fluid_2'=2,'solid'=8] {'fluid_1'}, use_global_device_ids=true, to_apply=%add.5 | all-reduce | flops 400 | bytes 3200
  223.2 0.2 dynamic-update-slice.12
  223.4 0.2 dynamic-update-slice.8
  223.7 8.5 %all-reduce.15 = (f32[100]{0:T(128)S(1)}, f32[100]{0:T(128)S(1)}) all-reduce(f32[100]{0:T(128)S(1)} %dynamic-update-slice.8, f32[100]{0:T(128)S(1)} %dynamic-update-slice.12), channel_id=12, replica_groups=mesh['fluid_0'=8,'fluid_1'=4,'fluid_2'=2,'solid'=8] {'fluid_2'}, use_global_device_ids=true, to_apply=%add.6 | all-reduce | flops 200 | bytes 1600
  232.4 0.2 dynamic-update-slice.13
  232.7 0.2 dynamic-update-slice.9
  232.9 11.2 %all-reduce.12 = (f32[400]{0:T(512)S(1)}, f32[400]{0:T(512)S(1)}) all-reduce(f32[400]{0:T(512)S(1)} %dynamic-update-slice.9, f32[400]{0:T(512)S(1)} %dynamic-update-slice.13), channel_id=13, replica_groups=mesh['fluid_0'=8,'fluid_1'=4,'fluid_2'=2,'solid'=8] {'solid'}, use_global_device_ids=true, to_apply=%add.7 | all-reduce | flops 800 | bytes 6400
  244.3 0.7 select_reduce_fusion.2
  245.9 4.6 %cholesky.55 = f32[50,50]{1,0:T(8,128)S(1)} custom-call(f32[50,50]{1,0:T(8,128)S(1)} %fusion.51), custom_call_target="Cholesky" | custom-call | tf_op jit(solution)/shard_map/jit(cholesky)/cholesky | solution.py:49
  250.5 0.6 compare_reduce_fusion
  251.2 0.7 fusion.48
  251.8 3.8 %custom-call.13 = f32[1,50,50]{1,2,0:T(8,128)S(1)} custom-call(f32[1,50,50]{2,1,0:T(8,128)S(1)} %fusion.48), custom_call_target="InvertDiagBlocksLowerTriangular" | custom-call | tf_op jit(solution)/shard_map/triangular_solve/custom-call.2 | solution.py:51
  256.2 0.3 fusion.14
  256.5 0.6 convert_bitcast_fusion
  257.1 21.1 %all_to_all.26 = bf16[64,4,3,128]{3,1,2,0:T(4,128)(2,1)S(1)} all-to-all(bf16[64,4,3,128]{3,1,2,0:T(4,128)(2,1)S(1)} %broadcast_in_dim.61), channel_id=1, replica_groups=mesh['fluid_0'=8,'fluid_1'=4,'fluid_2'=2,'solid'=8] {'fluid_0','fluid_1'..., dimensions={0} | all-to-all | bytes 393216 | tf_op jit(solution)/shard_map/all_to_all | solution.py:21
  278.3 0.2 convolution_convert_fusion.2
  278.5 0.7 convolution_multiply_fusion
  279.1 0.7 copy.102
  (93 shorter events, 3.5 us)
Async XLA Ops:
  0.6 85.3 %copy-start = (bf16[64,128,128]{2,1,0:T(8,128)(2,1)S(1)}, bf16[64,128,128]{2,1,0:T(8,128)(2,1)}, u32[]{:S(2)}) copy-start(bf16[64,128,128]{2,1,0:T(8,128)(2,1)} %param.17) | copy-start | bytes 6291460
  0.6 85.0 %copy-start.8 = (s32[64,1]{0,1:T(1,128)S(1)}, s32[64,1]{0,1:T(1,128)}, u32[]{:S(2)}) copy-start(s32[64,1]{0,1:T(1,128)} %param.19) | copy-start | bytes 772
  0.7 85.0 %copy-start.7 = (s32[64]{0:T(128)S(1)}, s32[64]{0:T(128)}, u32[]{:S(2)}) copy-start(s32[64]{0:T(128)} %param.20) | copy-start | bytes 772
  0.7 85.3 %copy-start.3 = (f32[64,3,128]{2,0,1:T(8,128)S(1)}, f32[64,3,128]{2,0,1:T(8,128)}, u32[]{:S(2)}) copy-start(f32[64,3,128]{2,0,1:T(8,128)} %param.15) | copy-start | bytes 294916
  0.7 85.3 %copy-start.4 = (f32[64,3,128]{2,0,1:T(8,128)S(1)}, f32[64,3,128]{2,0,1:T(8,128)}, u32[]{:S(2)}) copy-start(f32[64,3,128]{2,0,1:T(8,128)} %param.16) | copy-start | bytes 294916
  2.3 83.4 %all-to-all-start = ((bf16[64,4,3,128]{3,1,2,0:T(4,128)(2,1)}), bf16[64,4,3,128]{3,1,2,0:T(4,128)(2,1)S(1)}, u32[]{:S(2)}, u32[]{:S(2)}) async-start(bf16[64,4,3,128]{3,1,2,0:T(4,128)(2,1)} %broadcast_in_dim.50), calls=%async_computation | async-start | bytes 393216 | tf_op jit(solution)/shard_map/all_to_all | solution.py:21
  86.0 30.8 %copy-start.5 = (f32[1,4,3,128]{3,1,2,0:T(4,128)S(1)}, f32[1,4,3,128]{3,1,2,0:T(4,128)}, u32[]{:S(2)}) copy-start(f32[1,4,3,128]{3,1,2,0:T(4,128)} %param.21) | copy-start | bytes 18436
  86.0 30.8 %copy-start.6 = (f32[1,4,3,128]{3,1,2,0:T(4,128)S(1)}, f32[1,4,3,128]{3,1,2,0:T(4,128)}, u32[]{:S(2)}) copy-start(f32[1,4,3,128]{3,1,2,0:T(4,128)} %param.22) | copy-start | bytes 18436
  86.0 30.8 %copy-start.1 = (f32[50,1,4,3,128]{4,2,3,1,0:T(4,128)S(1)}, f32[50,1,4,3,128]{4,2,3,1,0:T(4,128)}, u32[]{:S(2)}) copy-start(f32[50,1,4,3,128]{4,2,3,1,0:T(4,128)} %param.23) | copy-start | bytes 921604
  87.7 73.4 %copy-start.2 = (f32[50,1,4,3,128]{4,2,3,1,0:T(4,128)S(1)}, f32[50,1,4,3,128]{4,2,3,1,0:T(4,128)}, u32[]{:S(2)}) copy-start(f32[50,1,4,3,128]{4,2,3,1,0:T(4,128)} %param.24) | copy-start | bytes 921604
  88.9 27.7 %all-to-all-start.1 = ((bf16[64,4,3,128]{3,1,2,0:T(4,128)(2,1)}), bf16[64,4,3,128]{3,1,2,0:T(4,128)(2,1)S(1)}, u32[]{:S(2)}, u32[]{:S(2)}) async-start(bf16[64,4,3,128]{3,1,2,0:T(4,128)(2,1)} %copy.85), calls=%async_computation.1 | async-start | bytes 393216 | tf_op jit(solution)/shard_map/all_to_all | solution.py:42
  185.9 16.9 %all-to-all-start.3 = ((bf16[64,4,3,128]{3,1,2,0:T(4,128)(2,1)}), bf16[64,4,3,128]{3,1,2,0:T(4,128)(2,1)S(1)}, u32[]{:S(2)}, u32[]{:S(2)}) async-start(bf16[64,4,3,128]{3,1,2,0:T(4,128)(2,1)} %copy.96), calls=%async_computation.3 | async-start | bytes 393216 | tf_op jit(solution)/shard_map/all_to_all | solution.py:42
